TPU v7x, 32 devices: a whole 2x2x4 slice. The times are simulated.
32 devices in a mesh: band: 8 (over z, core), lane: 4 (over y, x).
Axes of the slice: x: 2, y: 2, z: 4, core: 2. Of those that a mesh axis runs over, the one named last changes fastest.
Arguments:
- first_factor: bfloat16 [8192, 4096], P('band', 'lane'), may hold values from -6 to 6
- second_factor: bfloat16 [4096, 2048], P('band', 'lane'), may hold values from -0.09375 to 0.09375
- result_in: float32 [8192, 2048], P('band', 'lane'), may hold values from -6 to 6
- pivot_scale: float32 [4096], replicated, may hold values from 0.25 to 1.75
Outputs:
- updated: float32 [8192, 2048], P('band', 'lane')
All inputs are finite; a program needn't handle non-finite values.
Results may differ from a plain program's by a relative error of at most 0.002.
Values may be sent and summed in bfloat16 or wider, within the bound.
A program may use at most 128 MiB of HBM per device.

v0:
```python
import jax
import jax.numpy as jnp
from jax import lax
from jax.sharding import PartitionSpec as P


def join_panel(left_panel, right_panel):
    return jnp.dot(left_panel, right_panel, preferred_element_type=jnp.float32)


def on_device(first_factor, second_factor, result_in, pivot_scale):
    share = first_factor.shape[1]
    part_scale = lax.dynamic_slice_in_dim(pivot_scale, lax.axis_index("lane") * share, share)
    scaled_left = (first_factor.astype(jnp.float32) * part_scale).astype(jnp.bfloat16)
    left_line = lax.all_gather(scaled_left, "lane", axis=1, tiled=True)
    total = join_panel(left_line, lax.all_gather(second_factor, "band", axis=0, tiled=True))
    updated = result_in - total
    row_power = lax.psum(jnp.sum(updated * updated, axis=1), "lane")
    updated = (
        updated * lax.rsqrt(row_power / (updated.shape[1] * lax.axis_size("lane")) + 1e-06)[:, None]
    )
    return updated


def solution(mesh):
    return jax.shard_map(
        on_device,
        mesh=mesh,
        in_specs=(P("band", "lane"), P("band", "lane"), P("band", "lane"), P()),
        out_specs=P("band", "lane"),
        check_vma=False,
    )
```

profile of v0, /device:TPU:0, one launch (start us, length us, event | category | flops | bytes accessed | tf_op | source)
XLA Modules:
  0.0 177.2 jit_solution(5245780658395474004)
XLA Ops:
  6.5 0.0 all-gather.5.cloned.1.call-start
  6.5 0.7 all-gather.5.cloned.1.call-update
  7.3 0.0 all-gather.3.cloned.1.call-start
  7.3 0.7 dynamic_slice.3
  8.0 3.5 %multiply_convert_fusion = bf16[1024,1024]{1,0:T(8,128)(2,1)} fusion(bf16[1024,1024]{1,0:T(8,128)(2,1)} %param.4, f32[1024]{0:T(1024)S(1)} %dynamic_slice.3), kind=kLoop, calls=%fused_computation | loop fusion | flops 3145728 | bytes 4198400 | tf_op jit(solution)/shard_map/convert_element_type | solution.py:14
  11.5 0.0 copy-start
  11.5 0.0 all-gather.3.cloned.1.call-update
  11.5 1.6 copy-done
  13.1 1.8 %copy.5 = f32[1024,512]{0,1:T(8,128)} copy(f32[1024,512]{1,0:T(8,128)S(1)} %copy-done) | data formatting | bytes 4194304 | tf_op args[2]
  14.9 43.7 %all-gather.5.cloned.1.call-done = bf16[4096,512]{1,0:T(8,128)(2,1)} async-done(((bf16[512,512]{1,0:T(8,128)(2,1)}), bf16[4096,512]{1,0:T(8,128)(2,1)}) %all-gather.5.cloned.1.call-update) | async-done | bytes 4194320 | tf_op jit(solution)/shard_map/all_gather | solution.py:16
  58.6 88.2 %all-gather.3.cloned.1.call-done = bf16[1024,4096]{1,0:T(8,128)(2,1)} async-done(((bf16[1024,1024]{1,0:T(8,128)(2,1)}), bf16[1024,4096]{1,0:T(8,128)(2,1)}) %all-gather.3.cloned.1.call-update) | async-done | bytes 8388624 | tf_op jit(solution)/shard_map/all_gather | solution.py:15
  146.7 11.1 %multiply_reduce_fusion = (f32[1024]{0:T(1024)S(1)}, f32[1024,512]{0,1:T(8,128)}) fusion(f32[1024,512]{0,1:T(8,128)} %copy.5, bf16[1024,4096]{1,0:T(8,128)(2,1)} %all-gather.3.cloned.1.call-done, bf16[4096,512]{1,0:T(8,128)(2,1)} %all-gather.5.cloned.1.call-done), kind=kOutput, calls=%fused_computation.1 | convolution fusion | flops 4296539136 | bytes 16781312 | tf_op jit(solution)/shard_map/dot_general | solution.py:8
  157.8 8.9 %psum.7 = f32[1024]{0:T(1024)S(1)} all-reduce(f32[1024]{0:T(1024)S(1)} %get-tuple-element.5), channel_id=1, replica_groups=mesh['band'=8,'lane'=4] {'lane'}, use_global_device_ids=true, to_apply=%region_1.0 | all-reduce | flops 1024 | bytes 8192 | tf_op jit(solution)/shard_map/psum | solution.py:18
  166.7 1.8 %broadcast_multiply_fusion = f32[1024,512]{0,1:T(8,128)S(1)} fusion(f32[1024,512]{0,1:T(8,128)} %get-tuple-element.6, f32[1024]{0:T(1024)S(1)} %add_rsqrt_fusion), kind=kLoop, calls=%fused_computation.3 | loop fusion | flops 524288 | bytes 4198400 | tf_op jit(solution)/shard_map/mul | solution.py:20
  168.6 1.8 %copy.6 = f32[1024,512]{1,0:T(8,128)} copy(f32[1024,512]{0,1:T(8,128)S(1)} %broadcast_multiply_fusion) | data formatting | bytes 4194304 | tf_op jit(solution)/shard_map/mul | solution.py:20
  (1 shorter events, 0.0 us)
Async XLA Ops:
  6.5 52.0 %all-gather.5.cloned.1.call-start = ((), (), s32[]{:S(2)}) async-start(), calls=%async_computation.1 | async-start | bytes 4718592 | tf_op jit(solution)/shard_map/all_gather | solution.py:16
  7.3 139.5 %all-gather.3.cloned.1.call-start = ((), (), s32[]{:S(2)}) async-start(), calls=%async_computation | async-start | bytes 10485760 | tf_op jit(solution)/shard_map/all_gather | solution.py:15
  11.5 1.6 copy-start
Sparse Core Ops, SparseCore 0:
  8.9 49.5 all-gather.4
  60.4 86.2 all-gather.2
where the time goes:
time: 177 us
  waiting for transfers between devices  133 us (75%)
  between operations  13.4 us (8%)
  matrix products  11.1 us (6%)
  blocking collectives  8.9 us (5%)
  local copies, waits for them, and re-layouts  5.88 us (3%)
  other arithmetic  5.32 us (3%)
    all_gather x1, waiting for transfers between devices, on_device(): left_line = lax.all_gather(scaled_left, 'lane', axis=1, tiled=True)  88.2 us
    all_gather x1, waiting for transfers between devices, on_device(): lax.all_gather(second_factor, 'band', axis=0, tiled=True)  43.7 us
    dot_general x1, matrix products, join_panel(): return jnp.dot(left_panel, right_panel, preferred_element_type=jnp.float32)  11.1 us
    psum x1, blocking collectives, on_device(): row_power = lax.psum(jnp.sum(updated * updated, axis=1), 'lane')  8.9 us
  transfers between devices with their start and end apart: 2, of which 2 were waited for; matrix products, arithmetic and copies ran while one was open for 3% of the time, Pallas kernels for 0%

commit v1 on v0

--- a/solution.py
+++ b/solution.py
@@ -2,6 +2,18 @@
 import jax.numpy as jnp
 from jax import lax
 from jax.sharding import PartitionSpec as P
+from jax.lax import all_to_all, axis_size
+
+
+def ways_reach(vector):
+    devs = axis_size("band")
+    return all_to_all(
+        jnp.tile(vector, [devs if idx == 0 else 1 for idx in range(vector.ndim)]),
+        "band",
+        split_axis=0,
+        concat_axis=0,
+        tiled=True,
+    )
 
 
 def join_panel(left_panel, right_panel):
@@ -13,7 +25,7 @@
     part_scale = lax.dynamic_slice_in_dim(pivot_scale, lax.axis_index("lane") * share, share)
     scaled_left = (first_factor.astype(jnp.float32) * part_scale).astype(jnp.bfloat16)
     left_line = lax.all_gather(scaled_left, "lane", axis=1, tiled=True)
-    total = join_panel(left_line, lax.all_gather(second_factor, "band", axis=0, tiled=True))
+    total = join_panel(left_line, ways_reach(second_factor))
     updated = result_in - total
     row_power = lax.psum(jnp.sum(updated * updated, axis=1), "lane")
     updated = (

time: 177 us -> 146 us (0.82)
  waiting for transfers between devices: 133 us -> 92.3 us
  starting transfers between devices: 0.04 us -> 6.49 us
    all_to_all x0 -> x1, waiting for transfers between devices: none -> 92.3 us  [ways_reach(): all_to_all(jnp.tile(vector, [devs if idx == 0 else 1 for idx in range(vec...]
    all_gather x1, waiting for transfers between devices: 88.2 us -> 0.01 us  [on_device(): left_line = lax.all_gather(scaled_left, 'lane', axis=1, tiled=True)]
    all_gather x1 -> x0, waiting for transfers between devices: 43.7 us -> none  [on_device(): lax.all_gather(second_factor, 'band', axis=0, tiled=True)]
    all_to_all x0 -> x1, starting transfers between devices: none -> 6.49 us  [ways_reach(): all_to_all(jnp.tile(vector, [devs if idx == 0 else 1 for idx in range(vec...]
    another operation x0 -> x1, local copies, waits for them, and re-layouts: none -> 2.3 us  [ways_reach(): jnp.tile(vector, [devs if idx == 0 else 1 for idx in range(vector.ndim)])]
  transfers between devices with their start and end apart: 2 -> 2, of which waited for: 2 -> 1; matrix products, arithmetic and copies ran while one was open for 3% -> 3% of each run, Pallas kernels for 0% -> 0%
where the time goes in v1:
time: 146 us
  waiting for transfers between devices  92.3 us (63%)
  between operations  13.4 us (9%)
  matrix products  11.1 us (8%)
  blocking collectives  9.88 us (7%)
  local copies, waits for them, and re-layouts  7.64 us (5%)
  starting transfers between devices  6.49 us (4%)
  other arithmetic  5.32 us (4%)
    all_to_all x1, waiting for transfers between devices, ways_reach(): all_to_all(jnp.tile(vector, [devs if idx == 0 else 1 for idx in range(vec...  92.3 us
    dot_general x1, matrix products, join_panel(): return jnp.dot(left_panel, right_panel, preferred_element_type=jnp.float32)  11.1 us
    psum x1, blocking collectives, on_device(): row_power = lax.psum(jnp.sum(updated * updated, axis=1), 'lane')  9.88 us
    all_to_all x1, starting transfers between devices, ways_reach(): all_to_all(jnp.tile(vector, [devs if idx == 0 else 1 for idx in range(vec...  6.49 us
    convert_element_type x1, other arithmetic, on_device(): (first_factor.astype(jnp.float32) * part_scale).astype(jnp.bfloat16)  3.5 us
  transfers between devices with their start and end apart: 2, of which 1 were waited for; matrix products, arithmetic and copies ran while one was open for 3% of the time, Pallas kernels for 0%

profile of v1, /device:TPU:0, one launch (start us, length us, event | category | flops | bytes accessed | tf_op | source)
XLA Modules:
  0.0 146.1 jit_solution(2642336143959886845)
XLA Ops:
  6.5 0.0 all-gather.2.cloned.1.call-start
  6.5 0.7 dynamic_slice.3
  7.2 3.5 %multiply_convert_fusion = bf16[1024,1024]{1,0:T(8,128)(2,1)} fusion(bf16[1024,1024]{1,0:T(8,128)(2,1)} %param.4, f32[1024]{0:T(1024)S(1)} %dynamic_slice.3), kind=kLoop, calls=%fused_computation | loop fusion | flops 3145728 | bytes 4198400 | tf_op jit(solution)/shard_map/convert_element_type | solution.py:26
  10.7 0.0 copy-start.1
  10.7 0.0 all-gather.2.cloned.1.call-update
  10.7 1.0 copy-done.1
  11.8 2.3 %tile.2 = bf16[8,512,512]{2,1,0:T(8,128)(2,1)} broadcast(bf16[512,512]{1,0:T(8,128)(2,1)S(1)} %copy-done.1), dimensions={1,2} | broadcast | bytes 4718592 | tf_op jit(solution)/shard_map/tile | solution.py:11
  14.1 0.0 copy-start
  14.1 6.5 %all-to-all-start = ((bf16[8,512,512]{2,1,0:T(8,128)(2,1)}), bf16[8,512,512]{2,1,0:T(8,128)(2,1)}, u32[]{:S(2)}, u32[]{:S(2)}) async-start(bf16[8,512,512]{2,1,0:T(8,128)(2,1)} %tile.2), calls=%async_computation | async-start | bytes 8388608 | tf_op jit(solution)/shard_map/all_to_all | solution.py:10
  20.6 0.0 copy-done
  20.6 1.8 %copy.5 = f32[1024,512]{0,1:T(8,128)} copy(f32[1024,512]{1,0:T(8,128)S(1)} %copy-done) | data formatting | bytes 4194304 | tf_op args[2]
  22.4 92.3 %all-to-all-done = bf16[8,512,512]{2,1,0:T(8,128)(2,1)} async-done(((bf16[8,512,512]{2,1,0:T(8,128)(2,1)}), bf16[8,512,512]{2,1,0:T(8,128)(2,1)}, u32[]{:S(2)}, u32[]{:S(2)}) %all-to-all-start) | async-done | bytes 4194336 | tf_op jit(solution)/shard_map/all_to_all | solution.py:10
  114.6 0.0 all-gather.2.cloned.1.call-done
  114.6 11.1 %multiply_reduce_fusion = (f32[1024]{0:T(1024)S(1)}, f32[1024,512]{0,1:T(8,128)}) fusion(f32[1024,512]{0,1:T(8,128)} %copy.5, bf16[1024,4096]{1,0:T(8,128)(2,1)} %all-gather.2.cloned.1.call-done, bf16[4096,512]{1,0:T(8,128)(2,1)} %bitcast), kind=kOutput, calls=%fused_computation.1 | convolution fusion | flops 4296539136 | bytes 16781312 | tf_op jit(solution)/shard_map/dot_general | solution.py:20
  125.8 9.9 %psum.7 = f32[1024]{0:T(1024)S(1)} all-reduce(f32[1024]{0:T(1024)S(1)} %get-tuple-element.5), channel_id=1, replica_groups=mesh['band'=8,'lane'=4] {'lane'}, use_global_device_ids=true, to_apply=%region_1.0 | all-reduce | flops 1024 | bytes 8192 | tf_op jit(solution)/shard_map/psum | solution.py:30
  135.6 1.8 %broadcast_multiply_fusion = f32[1024,512]{0,1:T(8,128)S(1)} fusion(f32[1024,512]{0,1:T(8,128)} %get-tuple-element.6, f32[1024]{0:T(1024)S(1)} %add_rsqrt_fusion), kind=kLoop, calls=%fused_computation.3 | loop fusion | flops 524288 | bytes 4198400 | tf_op jit(solution)/shard_map/mul | solution.py:32
  137.5 1.8 %copy.6 = f32[1024,512]{1,0:T(8,128)} copy(f32[1024,512]{0,1:T(8,128)S(1)} %broadcast_multiply_fusion) | data formatting | bytes 4194304 | tf_op jit(solution)/shard_map/mul | solution.py:32
  (1 shorter events, 0.0 us)
Async XLA Ops:
  6.5 108.1 %all-gather.2.cloned.1.call-start = ((), (), s32[]{:S(2)}) async-start(), calls=%async_computation.1 | async-start | bytes 10485760 | tf_op jit(solution)/shard_map/all_gather | solution.py:27
  10.7 1.0 copy-start.1
  14.1 6.5 %copy-start = (f32[1024,512]{1,0:T(8,128)S(1)}, f32[1024,512]{1,0:T(8,128)}, u32[]{:S(2)}) copy-start(f32[1024,512]{1,0:T(8,128)} %param.6) | copy-start | bytes 6291460
  14.1 100.6 %all-to-all-start = ((bf16[8,512,512]{2,1,0:T(8,128)(2,1)}), bf16[8,512,512]{2,1,0:T(8,128)(2,1)}, u32[]{:S(2)}, u32[]{:S(2)}) async-start(bf16[8,512,512]{2,1,0:T(8,128)(2,1)} %tile.2), calls=%async_computation | async-start | bytes 8388608 | tf_op jit(solution)/shard_map/all_to_all | solution.py:10
Sparse Core Ops, SparseCore 0:
  10.9 90.1 all-gather.1
